TPU v7x, 32 devices: a whole 2x2x4 slice. The times are simulated.
32 devices in a mesh: expert: 8 (over z, y), mp: 4 (over x, core).
Axes of the slice: x: 2, y: 2, z: 4, core: 2. Of those that a mesh axis runs over, the one named last changes fastest.
Arguments:
- tokens: bfloat16 [1024, 3584], P('expert', 'mp'), may hold values from -6 to 6
- assignments: int32 [1024, 2], P('expert'), may hold values from 0 to 7, all different within a row; in each aligned block of 128 rows (0 to 127, 128 to 255, ...) at most 64 rows name the same one
- gate_probs: float32 [1024, 2], P('expert'), may hold values from 0.05 to 0.5
- expert_gate: bfloat16 [8, 3584, 2560], P('expert', None, 'mp'), may hold values from -0.09375 to 0.09375
- expert_up: bfloat16 [8, 3584, 2560], P('expert', None, 'mp'), may hold values from -0.09375 to 0.09375
- expert_down: bfloat16 [8, 2560, 3584], P('expert', 'mp'), may hold values from -0.125 to 0.125
- shared_gate: bfloat16 [3584, 10240], P('mp', 'expert'), may hold values from -0.09375 to 0.09375
- shared_up: bfloat16 [3584, 10240], P('mp', 'expert'), may hold values from -0.09375 to 0.09375
- shared_down_weight: bfloat16 [10240, 3584], P('expert', 'mp'), may hold values from -0.0625 to 0.0625
Outputs:
- layer_out: bfloat16 [1024, 3584], P('expert', 'mp')
Inputs may be any that keep to these rules, and one draw needn't show every extreme that they name: `assignments`: each row names 2 different experts; among the 128 rows of one index of the expert axis (aligned blocks) no expert is named more than 64 times.
All inputs are finite; a program needn't handle non-finite values.
Results may differ from a plain program's by a relative error of at most 0.0075.
Values may be sent and summed in bfloat16 or wider, within the bound.
No kernel may reach another device: no remote copies, remote signals or barrier semaphores. Data moves between devices by JAX's collectives and lax.ppermute only.
A program may use at most 128 MiB of HBM per device.

v0:
```python
import jax
import jax.numpy as jnp
from jax import lax
from jax.sharding import PartitionSpec as P


BF16 = jnp.bfloat16
F32 = jnp.float32


def bits_of(size):
    count = size.bit_length() - 1
    assert size == 1 << count
    return [1 << b for b in range(count)]


def dot(a, b):
    return jnp.dot(a, b, preferred_element_type=F32)


def three_parts(values):
    parts = []
    for _ in range(3):
        head = lax.reduce_precision(values, 8, 7)
        parts.append(head.astype(BF16))
        values = values - head
    return parts


def step(function, *values, after=()):
    held = lax.optimization_barrier(values + tuple(after))[: len(values)]
    return function(*held)


def on_device(
    tokens,
    assignments,
    gate_probs,
    expert_gate,
    expert_up,
    expert_down,
    shared_gate,
    shared_up,
    shared_down_weight,
):
    experts, parts = lax.axis_size("expert"), lax.axis_size("mp")
    expert, part = lax.axis_index("expert"), lax.axis_index("mp")
    rows, width = tokens.shape
    chosen = assignments.shape[1]
    slots = min(rows, max(2, 2 * rows * chosen // experts))
    expert_bits, part_bits = bits_of(experts), bits_of(parts)
    groups = [list(range(g, g + parts)) for g in range(0, experts, parts)]
    hidden_width = shared_gate.shape[1]

    def swap(value, de=0, dm=0):
        pairs = [
            (e * parts + m, (e ^ de) * parts + (m ^ dm))
            for e in range(experts)
            for m in range(parts)
        ]
        return lax.ppermute(value, ("expert", "mp"), pairs)

    def by_part(values):
        values = list(values)
        for bit in part_bits:
            flip = (part & bit) != 0
            values = [jnp.where(flip, values[j ^ bit], values[j]) for j in range(len(values))]
        return values

    def prepare(tokens, ids, probs):
        notes = [ids.T[k : k + 1].astype(BF16) for k in range(chosen)]
        for k in range(chosen):
            notes += three_parts(probs.T[k : k + 1])
        notes = jnp.concatenate(notes, axis=0)
        return jnp.concatenate([tokens, jnp.pad(notes, ((0, 0), (0, width - rows)))], axis=0)

    blocks = {0: step(prepare, tokens, assignments, gate_probs)}
    for bit in reversed(expert_bits[1:]):
        for k in list(blocks):
            blocks[k | bit] = swap(blocks[k], de=bit)
    for k in list(blocks):
        blocks[k | 1] = swap(blocks[k], de=1)

    slices = {0: tokens}
    for bit in part_bits[1:]:
        for j in list(slices):
            slices[j | bit] = swap(slices[j], dm=bit)
    others = [j for j in sorted(slices) if j]
    far = {0: jnp.concatenate([slices[j] for j in others], axis=1)}
    for bit in reversed(expert_bits):
        source = [k for k in sorted(far) if bit >= parts or k >= parts]
        if source:
            got = swap(jnp.stack([far[k] for k in source]), de=bit)
            for n, k in enumerate(source):
                far[k | bit] = got[n]

    before = jnp.triu(jnp.ones((rows, rows), F32), 1).astype(BF16)
    place = jnp.arange(slots, dtype=jnp.int32).astype(F32)[None, :, None]
    both = step(lambda a, b: jnp.concatenate([a, b], axis=1), shared_gate, shared_up)

    def pick(taking, *sources):
        return jnp.concatenate([dot(taking[i], b).astype(BF16) for i, b in enumerate(sources)])

    def dispatch(*members):
        table = jnp.stack([b[rows : rows + 4 * chosen, :rows] for b in members])
        ids = table[:, :chosen].astype(F32)
        probs = table[:, chosen:].astype(F32).reshape(len(members), chosen, 3, rows)
        probs = probs[:, :, 0] + (probs[:, :, 1] + probs[:, :, 2])
        mine = ids == expert.astype(F32)
        named = jnp.any(mine, axis=1).astype(F32)
        rank = dot(named.astype(BF16), before)
        taking = ((rank[:, None, :] == place) & (named[:, None, :] > 0)).astype(BF16)
        row_prob = jnp.sum(jnp.where(mine, probs, 0.0), axis=1)
        weight = jnp.sum(taking.astype(F32) * row_prob[:, None, :], axis=2)
        return pick(taking, *[b[:rows] for b in members]), weight, taking

    def shared_act(act, came):
        act = act + came.astype(F32)
        return (jax.nn.silu(act[:, :hidden_width]) * act[:, hidden_width:]).astype(BF16)

    def feed(own, core):
        gate_act = up_act = 0.0
        for j in sorted(range(parts), key=lambda j: j & 1):
            rows_j = core[j // 2] if j & 1 else own[j // 2]
            start = (part ^ j) * width
            gate_act += dot(rows_j, lax.dynamic_slice_in_dim(expert_gate[0], start, width, axis=0))
            up_act += dot(rows_j, lax.dynamic_slice_in_dim(expert_up[0], start, width, axis=0))
        return (jax.nn.silu(gate_act) * up_act).astype(BF16)

    def lower(js, kind):
        def function(hidden):
            out = []
            for j in js:
                columns = lax.dynamic_slice_in_dim(
                    expert_down[0], (part ^ j) * width, width, axis=1
                )
                out.append(dot(hidden, columns).astype(kind))
            return jnp.stack(out)

        return function

    odd = [j for j in range(parts) if j & 1]
    even = [j for j in range(parts) if not j & 1]
    total, routed_rows = {}, {}
    last_picked = last_act = last_left = last_weigh = ()
    for g, members in enumerate(groups):
        mine = [blocks[k] for k in members]
        picked, weight, taking = step(dispatch, *mine, after=last_picked)
        last_picked = (picked, weight, taking)

        slices = {0: picked}
        if g:
            picked_far = step(pick, taking, *[far[k] for k in members])
            for n, j in enumerate(others):
                slices[j] = picked_far[:, n * width : (n + 1) * width]
        else:
            for bit in part_bits[1:]:
                for j in list(slices):
                    slices[j | bit] = swap(slices[j], dm=bit)
        own = jnp.stack([slices[j] for j in even])
        core = swap(own, dm=1)

        held = step(lambda *b: tuple(by_part([x[:rows] for x in b])), *mine)

        def sums_of(js, kind):
            return lambda w, *h: dot(jnp.concatenate([h[j] for j in js]), w).astype(kind)

        leaving = step(sums_of(odd, BF16), both, *held)
        staying = step(sums_of(even, F32), both, *held)
        sums = {j: staying[i * rows : (i + 1) * rows] for i, j in enumerate(even)}
        pending = list(range(parts))
        for bit in part_bits:
            keep = [j for j in pending if not j & bit]
            if bit > 1:
                adds = [sums[j] for j in pending]

                def add(*v):
                    added = [x + y.astype(F32) for x, y in zip(v[::2], v[1::2])]
                    left = [x.astype(BF16) for x, j in zip(added, pending) if j & bit]
                    return jnp.concatenate(left), [x for x, j in zip(added, pending) if not j & bit]

                flat = [x for pair in adds for x in pair]
                leaving, stay = step(add, *flat, after=last_left)
                last_left = (leaving,)
                sums = dict(zip(keep, stay))
            came = swap(leaving, dm=bit)
            if 2 * bit == parts:
                break
            for i, j in enumerate(keep):
                sums[j] = (sums[j], came[i * rows : (i + 1) * rows])
            pending = keep
        act = step(shared_act, sums[0], came, after=last_act)
        last_act = (act,)

        known = {0: act}
        for bit in reversed(part_bits):
            order = sorted(known)
            got = swap(jnp.concatenate([known[j] for j in order]), dm=bit)
            for n, j in enumerate(order):
                known[j | bit] = got[n * rows : (n + 1) * rows]
        shared_hidden = step(lambda *v: tuple(by_part(v)), *[known[j] for j in range(parts)])

        hidden = step(feed, own, core)
        leaving = step(lower(odd, BF16), hidden)
        staying = step(lower(even, F32), hidden)
        partial = {j: staying[i] for i, j in enumerate(even)}
        pending = list(range(parts))
        for bit in part_bits:
            keep = [j for j in pending if not j & bit]
            if bit > 1:
                adds = [partial[j] for j in pending]

                def add_rows(*v):
                    added = [x + y.astype(F32) for x, y in zip(v[::2], v[1::2])]
                    left = [x.astype(BF16) for x, j in zip(added, pending) if j & bit]
                    return jnp.stack(left), [x for x, j in zip(added, pending) if not j & bit]

                flat = [x for pair in adds for x in pair]
                leaving, stay = step(add_rows, *flat, after=last_weigh)
                last_weigh = (leaving,)
                partial = dict(zip(keep, stay))
            came = swap(leaving, dm=bit)
            if 2 * bit < parts:
                for i, j in enumerate(keep):
                    partial[j] = (partial[j], came[i])
            pending = keep
        routed_rows[g] = (partial[0], came[0], weight, taking, shared_hidden)

    def weigh(result, came, weight):
        result = (result + came.astype(F32)).reshape(parts, slots, width)
        return (result * weight[:, :, None]).astype(BF16)

    def join(hidden, result, taking):
        routed = jnp.einsum("st,sd->td", taking, result, preferred_element_type=F32)
        return dot(hidden, shared_down_weight) + routed

    last_weigh = ()
    for g, members in reversed(list(enumerate(groups))):
        here, came, weight, taking, shared_hidden = routed_rows[g]
        result = step(weigh, here, came, weight, after=last_weigh)
        last_weigh = (result,)
        for i, k in enumerate(members):
            total[k] = join(shared_hidden[i], result[i], taking[i])

    left = list(range(experts))
    for bit in expert_bits:
        for k in sorted((k for k in left if k & bit), reverse=True):
            came = swap(total[k].astype(BF16), de=bit)
            total[k ^ bit] = total[k ^ bit] + came.astype(F32)
        left = [k for k in left if not k & bit]
    return total[0].astype(BF16)


def solution(mesh):
    in_specs = (
        P("expert", "mp"),
        P("expert", None),
        P("expert", None),
        P("expert", None, "mp"),
        P("expert", None, "mp"),
        P("expert", "mp", None),
        P("mp", "expert"),
        P("mp", "expert"),
        P("expert", "mp"),
    )
    out_specs = P("expert", "mp")
    return jax.shard_map(
        on_device, mesh=mesh, in_specs=in_specs, out_specs=out_specs, check_vma=False
    )
```

profile of v0, /device:TPU:0, one launch (start us, length us, event | category | flops | bytes accessed | tf_op | source)
XLA Modules:
  0.0 157.8 jit_solution(493232270889022749)
XLA Ops:
  0.0 3.0 %collective-permute-start.15 = (bf16[128,896]{1,0:T(8,128)(2,1)}, bf16[128,896]{1,0:T(8,128)(2,1)S(1)}, u32[]{:S(2)}, u32[]{:S(2)}) collective-permute-start(bf16[128,896]{1,0:T(8,128)(2,1)} %param.9), channel_id=1, source_target_pairs={{0,2},{1,3},{2,0},{3,1},{4,6},{5,7},{6,4},{7,5},{8,10},{9,11},{10,... | collective-permute-start | bytes 688136 | tf_op jit(solution)/shard_map/ppermute | solution.py:61
  3.0 0.7 convert_bitcast_fusion
  3.7 0.8 fusion.205
  4.4 1.0 fusion.143
  5.4 2.7 %collective-permute-start.11 = (bf16[136,896]{1,0:T(8,128)(2,1)S(1)}, bf16[136,896]{1,0:T(8,128)(2,1)S(1)}, u32[]{:S(2)}, u32[]{:S(2)}) collective-permute-start(bf16[136,896]{1,0:T(8,128)(2,1)S(1)} %fusion.143), channel_id=1, source_target_pairs={{0,16},{1,17},{2,18},{3,19},{4,20},{5,21},{6,22},{7,23},{8,24},{9,... | collective-permute-start | bytes 731144 | tf_op jit(solution)/shard_map/ppermute | solution.py:61
  8.1 1.6 collective-permute-start.1
  9.6 1.5 collective-permute-start
  11.2 2.0 %constant_dynamic-update-slice_fusion.1 = bf16[896,2560]{1,0:T(8,128)(2,1)S(1)} fusion(bf16[896,1280]{1,0:T(8,128)(2,1)} %param.15), kind=kLoop, calls=%fused_computation.296 | loop fusion | bytes 4587520
  13.6 6.1 %collective-permute-done.1 = bf16[136,896]{1,0:T(8,128)(2,1)S(1)} collective-permute-done((bf16[136,896]{1,0:T(8,128)(2,1)S(1)}, bf16[136,896]{1,0:T(8,128)(2,1)S(1)}, u32[]{:S(2)}, u32[]{:S(2)}) %collective-permute-start.1) | collective-permute-done | bytes 243744 | tf_op jit(solution)/shard_map/ppermute | solution.py:61
  19.6 1.5 collective-permute-start.2
  21.5 2.4 %collective-permute-start.13 = (bf16[136,896]{1,0:T(8,128)(2,1)S(1)}, bf16[136,896]{1,0:T(8,128)(2,1)S(1)}, u32[]{:S(2)}, u32[]{:S(2)}) collective-permute-start(bf16[136,896]{1,0:T(8,128)(2,1)S(1)} %collective-permute-done.11), channel_id=1, source_target_pairs={{0,8},{1,9},{2,10},{3,11},{4,12},{5,13},{6,14},{7,15},{8,0},{9,1},... | collective-permute-start | bytes 731144 | tf_op jit(solution)/shard_map/ppermute | solution.py:61
  24.4 4.5 %collective-permute-done.16 = bf16[1,128,896]{2,1,0:T(8,128)(2,1)S(1)} collective-permute-done((bf16[1,128,896]{2,1,0:T(8,128)(2,1)S(1)}, bf16[1,128,896]{2,1,0:T(8,128)(2,1)S(1)}, u32[]{:S(2)}, u32[]{:S(2)}) %collective-permute-start.16) | collective-permute-done | bytes 229408 | tf_op jit(solution)/shard_map/ppermute | solution.py:61
  28.9 0.6 collective-permute-start.17
  30.7 0.7 collective-permute-start.7
  31.6 1.5 convolution_convert_fusion.1
  33.2 1.5 fusion.73
  34.7 1.6 %collective-permute-start.14 = (bf16[136,896]{1,0:T(8,128)(2,1)S(1)}, bf16[136,896]{1,0:T(8,128)(2,1)S(1)}, u32[]{:S(2)}, u32[]{:S(2)}) collective-permute-start(bf16[136,896]{1,0:T(8,128)(2,1)S(1)} %collective-permute-done.13), channel_id=1, source_target_pairs={{0,4},{1,5},{2,6},{3,7},{4,0},{5,1},{6,2},{7,3},{8,12},{9,13},{10,... | collective-permute-start | bytes 731144 | tf_op jit(solution)/shard_map/ppermute | solution.py:61
  36.7 1.1 collective-permute-start.18
  37.8 5.7 %collective-permute-done.14 = bf16[136,896]{1,0:T(8,128)(2,1)S(1)} collective-permute-done((bf16[136,896]{1,0:T(8,128)(2,1)S(1)}, bf16[136,896]{1,0:T(8,128)(2,1)S(1)}, u32[]{:S(2)}, u32[]{:S(2)}) %collective-permute-start.14) | collective-permute-done | bytes 243744 | tf_op jit(solution)/shard_map/ppermute | solution.py:61
  44.9 1.5 convolution_convert_fusion
  46.6 1.5 fusion.80
  48.2 0.6 collective-permute-start.8
  48.8 4.1 %collective-permute-done.18 = bf16[2,128,896]{2,1,0:T(8,128)(2,1)S(1)} collective-permute-done((bf16[2,128,896]{2,1,0:T(8,128)(2,1)S(1)}, bf16[2,128,896]{2,1,0:T(8,128)(2,1)S(1)}, u32[]{:S(2)}, u32[]{:S(2)}) %collective-permute-start.18) | collective-permute-done | bytes 458784 | tf_op jit(solution)/shard_map/ppermute | solution.py:61
  54.3 1.4 collective-permute-start.4
  55.9 0.6 fusion.32
  56.5 0.6 fusion.42
  57.1 0.6 convolution_add_fusion.8
  57.7 0.6 convolution_add_fusion.11
  58.3 0.6 convolution_add_fusion.7
  58.8 0.6 convolution_add_fusion.10
  59.4 0.6 convolution_add_fusion.9
  60.0 0.6 fusion.2
  61.2 0.7 fusion.5
  64.3 1.4 collective-permute-start.26
  65.8 0.6 fusion.30
  66.4 0.6 fusion.40
  67.0 0.6 convolution_add_fusion.2
  67.5 0.6 convolution_add_fusion.5
  68.1 0.6 convolution_add_fusion.1
  68.7 0.6 convolution_add_fusion.4
  69.3 0.6 convolution_add_fusion.3
  69.8 0.6 fusion.3
  70.5 0.6 fusion.7
  73.2 0.7 collective-permute-start.5
  74.0 12.1 %collective-permute-done.26 = bf16[128,2560]{1,0:T(8,128)(2,1)S(1)} collective-permute-done((bf16[128,2560]{1,0:T(8,128)(2,1)S(1)}, bf16[128,2560]{1,0:T(8,128)(2,1)S(1)}, u32[]{:S(2)}, u32[]{:S(2)}) %collective-permute-start.26) | collective-permute-done | bytes 655392 | tf_op jit(solution)/shard_map/ppermute | solution.py:61
  86.4 1.4 collective-permute-start.27
  88.0 0.7 collective-permute-start.10
  88.7 4.3 %collective-permute-done.5 = bf16[128,1280]{1,0:T(8,128)(2,1)S(1)} collective-permute-done((bf16[128,1280]{1,0:T(8,128)(2,1)S(1)}, bf16[128,1280]{1,0:T(8,128)(2,1)S(1)}, u32[]{:S(2)}, u32[]{:S(2)}) %collective-permute-start.5) | collective-permute-done | bytes 327712 | tf_op jit(solution)/shard_map/ppermute | solution.py:61
  93.5 1.4 collective-permute-start.21
  95.0 5.1 %collective-permute-done.27 = bf16[128,1280]{1,0:T(8,128)(2,1)S(1)} collective-permute-done((bf16[128,1280]{1,0:T(8,128)(2,1)S(1)}, bf16[128,1280]{1,0:T(8,128)(2,1)S(1)}, u32[]{:S(2)}, u32[]{:S(2)}) %collective-permute-start.27) | collective-permute-done | bytes 327712 | tf_op jit(solution)/shard_map/ppermute | solution.py:61
  100.3 0.6 fusion.127
  102.0 0.6 fusion.133
  102.5 16.7 %collective-permute-done.21 = bf16[1,256,896]{2,1,0:T(8,128)(2,1)S(1)} collective-permute-done((bf16[1,256,896]{2,1,0:T(8,128)(2,1)S(1)}, bf16[1,256,896]{2,1,0:T(8,128)(2,1)S(1)}, u32[]{:S(2)}, u32[]{:S(2)}) %collective-permute-start.21) | collective-permute-done | bytes 458784 | tf_op jit(solution)/shard_map/ppermute | solution.py:61
  120.0 1.8 %collective-permute-start.23 = (bf16[128,896]{1,0:T(8,128)(2,1)S(1)}, bf16[128,896]{1,0:T(8,128)(2,1)S(1)}, u32[]{:S(2)}, u32[]{:S(2)}) collective-permute-start(bf16[128,896]{1,0:T(8,128)(2,1)S(1)} %fusion.9), channel_id=1, source_target_pairs={{0,4},{1,5},{2,6},{3,7},{4,0},{5,1},{6,2},{7,3},{8,12},{9,13},{10,... | collective-permute-start | bytes 688136 | tf_op jit(solution)/shard_map/ppermute | solution.py:61
  122.1 0.6 collective-permute-start.22
  122.7 6.1 %collective-permute-done.23 = bf16[128,896]{1,0:T(8,128)(2,1)S(1)} collective-permute-done((bf16[128,896]{1,0:T(8,128)(2,1)S(1)}, bf16[128,896]{1,0:T(8,128)(2,1)S(1)}, u32[]{:S(2)}, u32[]{:S(2)}) %collective-permute-start.23) | collective-permute-done | bytes 229408 | tf_op jit(solution)/shard_map/ppermute | solution.py:61
  129.1 1.5 collective-permute-start.24
  132.5 1.6 %collective-permute-start.30 = (bf16[128,896]{1,0:T(8,128)(2,1)S(1)}, bf16[128,896]{1,0:T(8,128)(2,1)S(1)}, u32[]{:S(2)}, u32[]{:S(2)}) collective-permute-start(bf16[128,896]{1,0:T(8,128)(2,1)S(1)} %fusion.11), channel_id=1, source_target_pairs={{0,4},{1,5},{2,6},{3,7},{4,0},{5,1},{6,2},{7,3},{8,12},{9,13},{10,... | collective-permute-start | bytes 688136 | tf_op jit(solution)/shard_map/ppermute | solution.py:61
  135.4 4.3 %collective-permute-done.30 = bf16[128,896]{1,0:T(8,128)(2,1)S(1)} collective-permute-done((bf16[128,896]{1,0:T(8,128)(2,1)S(1)}, bf16[128,896]{1,0:T(8,128)(2,1)S(1)}, u32[]{:S(2)}, u32[]{:S(2)}) %collective-permute-start.30) | collective-permute-done | bytes 229408 | tf_op jit(solution)/shard_map/ppermute | solution.py:61
  140.0 1.5 collective-permute-start.31
  142.2 4.0 %collective-permute-done.31 = bf16[128,896]{1,0:T(8,128)(2,1)S(1)} collective-permute-done((bf16[128,896]{1,0:T(8,128)(2,1)S(1)}, bf16[128,896]{1,0:T(8,128)(2,1)S(1)}, u32[]{:S(2)}, u32[]{:S(2)}) %collective-permute-start.31) | collective-permute-done | bytes 229408 | tf_op jit(solution)/shard_map/ppermute | solution.py:61
  146.3 4.3 %collective-permute-start.32 = (bf16[128,896]{1,0:T(8,128)(2,1)S(1)}, bf16[128,896]{1,0:T(8,128)(2,1)S(1)}, u32[]{:S(2)}, u32[]{:S(2)}) collective-permute-start(bf16[128,896]{1,0:T(8,128)(2,1)S(1)} %add_convert_fusion.5), channel_id=1, source_target_pairs={{0,16},{1,17},{2,18},{3,19},{4,20},{5,21},{6,22},{7,23},{8,24},{9,... | collective-permute-start | bytes 688136 | tf_op jit(solution)/shard_map/ppermute | solution.py:61
  150.9 6.2 %collective-permute-done.32 = bf16[128,896]{1,0:T(8,128)(2,1)S(1)} collective-permute-done((bf16[128,896]{1,0:T(8,128)(2,1)S(1)}, bf16[128,896]{1,0:T(8,128)(2,1)S(1)}, u32[]{:S(2)}, u32[]{:S(2)}) %collective-permute-start.32) | collective-permute-done | bytes 229408 | tf_op jit(solution)/shard_map/ppermute | solution.py:61
  157.0 0.8 add_convert_fusion.4
  (146 shorter events, 19.2 us)
Async XLA Ops:
  0.0 100.3 %copy-start = (bf16[1280,896]{1,0:T(8,128)(2,1)S(1)}, bf16[1280,896]{1,0:T(8,128)(2,1)}, u32[]{:S(2)}) copy-start(bf16[1280,896]{1,0:T(8,128)(2,1)} %param.17) | copy-start | bytes 6881284
  0.0 13.1 %collective-permute-start.15 = (bf16[128,896]{1,0:T(8,128)(2,1)}, bf16[128,896]{1,0:T(8,128)(2,1)S(1)}, u32[]{:S(2)}, u32[]{:S(2)}) collective-permute-start(bf16[128,896]{1,0:T(8,128)(2,1)} %param.9), channel_id=1, source_target_pairs={{0,2},{1,3},{2,0},{3,1},{4,6},{5,7},{6,4},{7,5},{8,10},{9,11},{10,... | collective-permute-start | bytes 688136 | tf_op jit(solution)/shard_map/ppermute | solution.py:61
  5.4 16.1 %collective-permute-start.11 = (bf16[136,896]{1,0:T(8,128)(2,1)S(1)}, bf16[136,896]{1,0:T(8,128)(2,1)S(1)}, u32[]{:S(2)}, u32[]{:S(2)}) collective-permute-start(bf16[136,896]{1,0:T(8,128)(2,1)S(1)} %fusion.143), channel_id=1, source_target_pairs={{0,16},{1,17},{2,18},{3,19},{4,20},{5,21},{6,22},{7,23},{8,24},{9,... | collective-permute-start | bytes 731144 | tf_op jit(solution)/shard_map/ppermute | solution.py:61
  8.1 11.6 %collective-permute-start.1 = (bf16[136,896]{1,0:T(8,128)(2,1)S(1)}, bf16[136,896]{1,0:T(8,128)(2,1)S(1)}, u32[]{:S(2)}, u32[]{:S(2)}) collective-permute-start(bf16[136,896]{1,0:T(8,128)(2,1)S(1)} %fusion.143), channel_id=1, source_target_pairs={{0,8},{1,9},{2,10},{3,11},{4,12},{5,13},{6,14},{7,15},{8,0},{9,1},... | collective-permute-start | bytes 731144 | tf_op jit(solution)/shard_map/ppermute | solution.py:61
  9.6 19.9 %collective-permute-start = (bf16[136,896]{1,0:T(8,128)(2,1)S(1)}, bf16[136,896]{1,0:T(8,128)(2,1)S(1)}, u32[]{:S(2)}, u32[]{:S(2)}) collective-permute-start(bf16[136,896]{1,0:T(8,128)(2,1)S(1)} %fusion.143), channel_id=1, source_target_pairs={{0,4},{1,5},{2,6},{3,7},{4,0},{5,1},{6,2},{7,3},{8,12},{9,13},{10,... | collective-permute-start | bytes 731144 | tf_op jit(solution)/shard_map/ppermute | solution.py:61
  11.2 10.0 %copy-start.1 = (bf16[896,1280]{1,0:T(8,128)(2,1)S(1)}, bf16[896,1280]{1,0:T(8,128)(2,1)}, u32[]{:S(2)}) copy-start(bf16[896,1280]{1,0:T(8,128)(2,1)} %param.16) | copy-start | bytes 6881284
  13.1 15.8 %collective-permute-start.16 = (bf16[1,128,896]{2,1,0:T(8,128)(2,1)S(1)}, bf16[1,128,896]{2,1,0:T(8,128)(2,1)S(1)}, u32[]{:S(2)}, u32[]{:S(2)}) collective-permute-start(bf16[1,128,896]{2,1,0:T(8,128)(2,1)S(1)} %bitcast.283), channel_id=1, source_target_pairs={{0,16},{1,17},{2,18},{3,19},{4,20},{5,21},{6,22},{7,23},{8,24},{9,... | collective-permute-start | bytes 688136 | tf_op jit(solution)/shard_map/ppermute | solution.py:61
  19.6 9.9 %collective-permute-start.2 = (bf16[136,896]{1,0:T(8,128)(2,1)S(1)}, bf16[136,896]{1,0:T(8,128)(2,1)S(1)}, u32[]{:S(2)}, u32[]{:S(2)}) collective-permute-start(bf16[136,896]{1,0:T(8,128)(2,1)S(1)} %collective-permute-done.1), channel_id=1, source_target_pairs={{0,4},{1,5},{2,6},{3,7},{4,0},{5,1},{6,2},{7,3},{8,12},{9,13},{10,... | collective-permute-start | bytes 731144 | tf_op jit(solution)/shard_map/ppermute | solution.py:61
  21.5 13.2 %collective-permute-start.13 = (bf16[136,896]{1,0:T(8,128)(2,1)S(1)}, bf16[136,896]{1,0:T(8,128)(2,1)S(1)}, u32[]{:S(2)}, u32[]{:S(2)}) collective-permute-start(bf16[136,896]{1,0:T(8,128)(2,1)S(1)} %collective-permute-done.11), channel_id=1, source_target_pairs={{0,8},{1,9},{2,10},{3,11},{4,12},{5,13},{6,14},{7,15},{8,0},{9,1},... | collective-permute-start | bytes 731144 | tf_op jit(solution)/shard_map/ppermute | solution.py:61
  23.9 14.0 %collective-permute-start.12 = (bf16[136,896]{1,0:T(8,128)(2,1)S(1)}, bf16[136,896]{1,0:T(8,128)(2,1)S(1)}, u32[]{:S(2)}, u32[]{:S(2)}) collective-permute-start(bf16[136,896]{1,0:T(8,128)(2,1)S(1)} %collective-permute-done.11), channel_id=1, source_target_pairs={{0,4},{1,5},{2,6},{3,7},{4,0},{5,1},{6,2},{7,3},{8,12},{9,13},{10,... | collective-permute-start | bytes 731144 | tf_op jit(solution)/shard_map/ppermute | solution.py:61
  28.9 7.7 %collective-permute-start.17 = (bf16[1,128,896]{2,1,0:T(8,128)(2,1)S(1)}, bf16[1,128,896]{2,1,0:T(8,128)(2,1)S(1)}, u32[]{:S(2)}, u32[]{:S(2)}) collective-permute-start(bf16[1,128,896]{2,1,0:T(8,128)(2,1)S(1)} %collective-permute-done.16), channel_id=1, source_target_pairs={{0,8},{1,9},{2,10},{3,11},{4,12},{5,13},{6,14},{7,15},{8,0},{9,1},... | collective-permute-start | bytes 688136 | tf_op jit(solution)/shard_map/ppermute | solution.py:61
  30.7 17.4 %collective-permute-start.7 = (bf16[256,896]{1,0:T(8,128)(2,1)S(1)}, bf16[256,896]{1,0:T(8,128)(2,1)S(1)}, u32[]{:S(2)}, u32[]{:S(2)}) collective-permute-start(bf16[256,896]{1,0:T(8,128)(2,1)S(1)} %get-tuple-element.174), channel_id=1, source_target_pairs={{0,2},{1,3},{2,0},{3,1},{4,6},{5,7},{6,4},{7,5},{8,10},{9,11},{10,... | collective-permute-start | bytes 1376264 | tf_op jit(solution)/shard_map/ppermute | solution.py:61
  33.1 20.8 %collective-permute-start.3 = (bf16[256,2560]{1,0:T(8,128)(2,1)S(1)}, bf16[256,2560]{1,0:T(8,128)(2,1)S(1)}, u32[]{:S(2)}, u32[]{:S(2)}) collective-permute-start(bf16[256,2560]{1,0:T(8,128)(2,1)S(1)} %convolution_convert_fusion.1), channel_id=1, source_target_pairs={{0,1},{1,0},{2,3},{3,2},{4,5},{5,4},{6,7},{7,6},{8,9},{9,8},{10,11... | collective-permute-start | bytes 3932168 | tf_op jit(solution)/shard_map/ppermute | solution.py:61
  34.7 8.8 %collective-permute-start.14 = (bf16[136,896]{1,0:T(8,128)(2,1)S(1)}, bf16[136,896]{1,0:T(8,128)(2,1)S(1)}, u32[]{:S(2)}, u32[]{:S(2)}) collective-permute-start(bf16[136,896]{1,0:T(8,128)(2,1)S(1)} %collective-permute-done.13), channel_id=1, source_target_pairs={{0,4},{1,5},{2,6},{3,7},{4,0},{5,1},{6,2},{7,3},{8,12},{9,13},{10,... | collective-permute-start | bytes 731144 | tf_op jit(solution)/shard_map/ppermute | solution.py:61
  36.7 16.2 %collective-permute-start.18 = (bf16[2,128,896]{2,1,0:T(8,128)(2,1)S(1)}, bf16[2,128,896]{2,1,0:T(8,128)(2,1)S(1)}, u32[]{:S(2)}, u32[]{:S(2)}) collective-permute-start(bf16[2,128,896]{2,1,0:T(8,128)(2,1)S(1)} %pad_maximum_fusion.7), channel_id=1, source_target_pairs={{0,4},{1,5},{2,6},{3,7},{4,0},{5,1},{6,2},{7,3},{8,12},{9,13},{10,... | collective-permute-start | bytes 1376264 | tf_op jit(solution)/shard_map/ppermute | solution.py:61
  46.5 17.6 %collective-permute-start.25 = (bf16[256,2560]{1,0:T(8,128)(2,1)S(1)}, bf16[256,2560]{1,0:T(8,128)(2,1)S(1)}, u32[]{:S(2)}, u32[]{:S(2)}) collective-permute-start(bf16[256,2560]{1,0:T(8,128)(2,1)S(1)} %convolution_convert_fusion), channel_id=1, source_target_pairs={{0,1},{1,0},{2,3},{3,2},{4,5},{5,4},{6,7},{7,6},{8,9},{9,8},{10,11... | collective-permute-start | bytes 3932168 | tf_op jit(solution)/shard_map/ppermute | solution.py:61
  46.6 9.3 %slice-start.4 = ((s8[4587520]{0:T(1024)(128)(4,1)}), s8[4194304]{0:T(1024)(128)(4,1)S(1)}, s32[]{:S(2)}) async-start(s8[4587520]{0:T(1024)(128)(4,1)} %bitcast.271), calls=%async_computation.4 | async-start | bytes 8388608
  48.2 7.7 %collective-permute-start.8 = (bf16[2,256,896]{2,1,0:T(8,128)(2,1)S(1)}, bf16[2,256,896]{2,1,0:T(8,128)(2,1)S(1)}, u32[]{:S(2)}, u32[]{:S(2)}) collective-permute-start(bf16[2,256,896]{2,1,0:T(8,128)(2,1)S(1)} %pad_maximum_fusion), channel_id=1, source_target_pairs={{0,1},{1,0},{2,3},{3,2},{4,5},{5,4},{6,7},{7,6},{8,9},{9,8},{10,11... | collective-permute-start | bytes 2752520 | tf_op jit(solution)/shard_map/ppermute | solution.py:61
  53.5 2.4 %slice-start.5 = ((s8[4587520]{0:T(1024)(128)(4,1)}), s8[393216]{0:T(1024)(128)(4,1)S(1)}, s32[]{:S(2)}) async-start(s8[4587520]{0:T(1024)(128)(4,1)} %bitcast.271), calls=%async_computation.5 | async-start | bytes 786432
  53.8 12.0 %collective-permute-start.19 = (bf16[2,256,896]{2,1,0:T(8,128)(2,1)S(1)}, bf16[2,256,896]{2,1,0:T(8,128)(2,1)S(1)}, u32[]{:S(2)}, u32[]{:S(2)}) collective-permute-start(bf16[2,256,896]{2,1,0:T(8,128)(2,1)S(1)} %pad_maximum_fusion.2), channel_id=1, source_target_pairs={{0,1},{1,0},{2,3},{3,2},{4,5},{5,4},{6,7},{7,6},{8,9},{9,8},{10,11... | collective-permute-start | bytes 2752520 | tf_op jit(solution)/shard_map/ppermute | solution.py:61
  54.0 2.5 %slice-start = ((s8[4587520]{0:T(1024)(128)(4,1)}), s8[4194304]{0:T(1024)(128)(4,1)S(1)}, s32[]{:S(2)}) async-start(s8[4587520]{0:T(1024)(128)(4,1)} %bitcast.267), calls=%async_computation | async-start | bytes 8388608
  54.0 2.5 %slice-start.1 = ((s8[4587520]{0:T(1024)(128)(4,1)}), s8[393216]{0:T(1024)(128)(4,1)S(1)}, s32[]{:S(2)}) async-start(s8[4587520]{0:T(1024)(128)(4,1)} %bitcast.267), calls=%async_computation.1 | async-start | bytes 786432
  54.3 18.6 %collective-permute-start.4 = (bf16[128,2560]{1,0:T(8,128)(2,1)S(1)}, bf16[128,2560]{1,0:T(8,128)(2,1)S(1)}, u32[]{:S(2)}, u32[]{:S(2)}) collective-permute-start(bf16[128,2560]{1,0:T(8,128)(2,1)S(1)} %get-tuple-element.195), channel_id=1, source_target_pairs={{0,2},{1,3},{2,0},{3,1},{4,6},{5,7},{6,4},{7,5},{8,10},{9,11},{10,... | collective-permute-start | bytes 1966088 | tf_op jit(solution)/shard_map/ppermute | solution.py:61
  58.8 2.2 %slice-start.2 = ((s8[4587520]{0:T(1024)(128)(4,1)}), s8[4194304]{0:T(1024)(128)(4,1)S(1)}, s32[]{:S(2)}) async-start(s8[4587520]{0:T(1024)(128)(4,1)} %bitcast.269), calls=%async_computation.2 | async-start | bytes 8388608
  59.4 1.8 %slice-start.3 = ((s8[4587520]{0:T(1024)(128)(4,1)}), s8[393216]{0:T(1024)(128)(4,1)S(1)}, s32[]{:S(2)}) async-start(s8[4587520]{0:T(1024)(128)(4,1)} %bitcast.269), calls=%async_computation.3 | async-start | bytes 786432
  62.6 25.2 %collective-permute-start.9 = (bf16[2,256,896]{2,1,0:T(8,128)(2,1)S(1)}, bf16[2,256,896]{2,1,0:T(8,128)(2,1)S(1)}, u32[]{:S(2)}, u32[]{:S(2)}) collective-permute-start(bf16[2,256,896]{2,1,0:T(8,128)(2,1)S(1)} %pad_maximum_fusion.1), channel_id=1, source_target_pairs={{0,1},{1,0},{2,3},{3,2},{4,5},{5,4},{6,7},{7,6},{8,9},{9,8},{10,11... | collective-permute-start | bytes 2752520 | tf_op jit(solution)/shard_map/ppermute | solution.py:61
  64.3 21.8 %collective-permute-start.26 = (bf16[128,2560]{1,0:T(8,128)(2,1)S(1)}, bf16[128,2560]{1,0:T(8,128)(2,1)S(1)}, u32[]{:S(2)}, u32[]{:S(2)}) collective-permute-start(bf16[128,2560]{1,0:T(8,128)(2,1)S(1)} %add_convert_fusion), channel_id=1, source_target_pairs={{0,2},{1,3},{2,0},{3,1},{4,6},{5,7},{6,4},{7,5},{8,10},{9,11},{10,... | collective-permute-start | bytes 1966088 | tf_op jit(solution)/shard_map/ppermute | solution.py:61
  71.7 21.6 %collective-permute-start.20 = (bf16[2,256,896]{2,1,0:T(8,128)(2,1)S(1)}, bf16[2,256,896]{2,1,0:T(8,128)(2,1)S(1)}, u32[]{:S(2)}, u32[]{:S(2)}) collective-permute-start(bf16[2,256,896]{2,1,0:T(8,128)(2,1)S(1)} %pad_maximum_fusion.3), channel_id=1, source_target_pairs={{0,1},{1,0},{2,3},{3,2},{4,5},{5,4},{6,7},{7,6},{8,9},{9,8},{10,11... | collective-permute-start | bytes 2752520 | tf_op jit(solution)/shard_map/ppermute | solution.py:61
  73.2 19.8 %collective-permute-start.5 = (bf16[128,1280]{1,0:T(8,128)(2,1)S(1)}, bf16[128,1280]{1,0:T(8,128)(2,1)S(1)}, u32[]{:S(2)}, u32[]{:S(2)}) collective-permute-start(bf16[128,1280]{1,0:T(8,128)(2,1)S(1)} %fusion.69), channel_id=1, source_target_pairs={{0,2},{1,3},{2,0},{3,1},{4,6},{5,7},{6,4},{7,5},{8,10},{9,11},{10,... | collective-permute-start | bytes 983048 | tf_op jit(solution)/shard_map/ppermute | solution.py:61
  86.4 13.7 %collective-permute-start.27 = (bf16[128,1280]{1,0:T(8,128)(2,1)S(1)}, bf16[128,1280]{1,0:T(8,128)(2,1)S(1)}, u32[]{:S(2)}, u32[]{:S(2)}) collective-permute-start(bf16[128,1280]{1,0:T(8,128)(2,1)S(1)} %fusion.68), channel_id=1, source_target_pairs={{0,2},{1,3},{2,0},{3,1},{4,6},{5,7},{6,4},{7,5},{8,10},{9,11},{10,... | collective-permute-start | bytes 983048 | tf_op jit(solution)/shard_map/ppermute | solution.py:61
  88.0 31.5 %collective-permute-start.10 = (bf16[1,256,896]{2,1,0:T(8,128)(2,1)S(1)}, bf16[1,256,896]{2,1,0:T(8,128)(2,1)S(1)}, u32[]{:S(2)}, u32[]{:S(2)}) collective-permute-start(bf16[1,256,896]{2,1,0:T(8,128)(2,1)S(1)} %fusion.71), channel_id=1, source_target_pairs={{0,2},{1,3},{2,0},{3,1},{4,6},{5,7},{6,4},{7,5},{8,10},{9,11},{10,... | collective-permute-start | bytes 1376264 | tf_op jit(solution)/shard_map/ppermute | solution.py:61
  93.1 7.1 %collective-permute-start.6 = (bf16[256,1280]{1,0:T(8,128)(2,1)S(1)}, bf16[256,1280]{1,0:T(8,128)(2,1)S(1)}, u32[]{:S(2)}, u32[]{:S(2)}) collective-permute-start(bf16[256,1280]{1,0:T(8,128)(2,1)S(1)} %pad_maximum_fusion.4), channel_id=1, source_target_pairs={{0,1},{1,0},{2,3},{3,2},{4,5},{5,4},{6,7},{7,6},{8,9},{9,8},{10,11... | collective-permute-start | bytes 1966088 | tf_op jit(solution)/shard_map/ppermute | solution.py:61
  93.5 25.8 %collective-permute-start.21 = (bf16[1,256,896]{2,1,0:T(8,128)(2,1)S(1)}, bf16[1,256,896]{2,1,0:T(8,128)(2,1)S(1)}, u32[]{:S(2)}, u32[]{:S(2)}) collective-permute-start(bf16[1,256,896]{2,1,0:T(8,128)(2,1)S(1)} %fusion.72), channel_id=1, source_target_pairs={{0,2},{1,3},{2,0},{3,1},{4,6},{5,7},{6,4},{7,5},{8,10},{9,11},{10,... | collective-permute-start | bytes 1376264 | tf_op jit(solution)/shard_map/ppermute | solution.py:61
  100.1 30.4 %collective-permute-start.28 = (bf16[256,1280]{1,0:T(8,128)(2,1)S(1)}, bf16[256,1280]{1,0:T(8,128)(2,1)S(1)}, u32[]{:S(2)}, u32[]{:S(2)}) collective-permute-start(bf16[256,1280]{1,0:T(8,128)(2,1)S(1)} %pad_maximum_fusion.5), channel_id=1, source_target_pairs={{0,1},{1,0},{2,3},{3,2},{4,5},{5,4},{6,7},{7,6},{8,9},{9,8},{10,11... | collective-permute-start | bytes 1966088 | tf_op jit(solution)/shard_map/ppermute | solution.py:61
  120.0 8.8 %collective-permute-start.23 = (bf16[128,896]{1,0:T(8,128)(2,1)S(1)}, bf16[128,896]{1,0:T(8,128)(2,1)S(1)}, u32[]{:S(2)}, u32[]{:S(2)}) collective-permute-start(bf16[128,896]{1,0:T(8,128)(2,1)S(1)} %fusion.9), channel_id=1, source_target_pairs={{0,4},{1,5},{2,6},{3,7},{4,0},{5,1},{6,2},{7,3},{8,12},{9,13},{10,... | collective-permute-start | bytes 688136 | tf_op jit(solution)/shard_map/ppermute | solution.py:61
  122.1 28.7 %collective-permute-start.22 = (bf16[128,896]{1,0:T(8,128)(2,1)S(1)}, bf16[128,896]{1,0:T(8,128)(2,1)S(1)}, u32[]{:S(2)}, u32[]{:S(2)}) collective-permute-start(bf16[128,896]{1,0:T(8,128)(2,1)S(1)} %fusion.8), channel_id=1, source_target_pairs={{0,4},{1,5},{2,6},{3,7},{4,0},{5,1},{6,2},{7,3},{8,12},{9,13},{10,... | collective-permute-start | bytes 688136 | tf_op jit(solution)/shard_map/ppermute | solution.py:61
  129.1 21.8 %collective-permute-start.24 = (bf16[128,896]{1,0:T(8,128)(2,1)S(1)}, bf16[128,896]{1,0:T(8,128)(2,1)S(1)}, u32[]{:S(2)}, u32[]{:S(2)}) collective-permute-start(bf16[128,896]{1,0:T(8,128)(2,1)S(1)} %add_convert_fusion.7), channel_id=1, source_target_pairs={{0,8},{1,9},{2,10},{3,11},{4,12},{5,13},{6,14},{7,15},{8,0},{9,1},... | collective-permute-start | bytes 688136 | tf_op jit(solution)/shard_map/ppermute | solution.py:61
  132.5 7.3 %collective-permute-start.30 = (bf16[128,896]{1,0:T(8,128)(2,1)S(1)}, bf16[128,896]{1,0:T(8,128)(2,1)S(1)}, u32[]{:S(2)}, u32[]{:S(2)}) collective-permute-start(bf16[128,896]{1,0:T(8,128)(2,1)S(1)} %fusion.11), channel_id=1, source_target_pairs={{0,4},{1,5},{2,6},{3,7},{4,0},{5,1},{6,2},{7,3},{8,12},{9,13},{10,... | collective-permute-start | bytes 688136 | tf_op jit(solution)/shard_map/ppermute | solution.py:61
  134.4 7.8 %collective-permute-start.29 = (bf16[128,896]{1,0:T(8,128)(2,1)S(1)}, bf16[128,896]{1,0:T(8,128)(2,1)S(1)}, u32[]{:S(2)}, u32[]{:S(2)}) collective-permute-start(bf16[128,896]{1,0:T(8,128)(2,1)S(1)} %fusion.10), channel_id=1, source_target_pairs={{0,4},{1,5},{2,6},{3,7},{4,0},{5,1},{6,2},{7,3},{8,12},{9,13},{10,... | collective-permute-start | bytes 688136 | tf_op jit(solution)/shard_map/ppermute | solution.py:61
  140.0 6.2 %collective-permute-start.31 = (bf16[128,896]{1,0:T(8,128)(2,1)S(1)}, bf16[128,896]{1,0:T(8,128)(2,1)S(1)}, u32[]{:S(2)}, u32[]{:S(2)}) collective-permute-start(bf16[128,896]{1,0:T(8,128)(2,1)S(1)} %add_convert_fusion.6), channel_id=1, source_target_pairs={{0,8},{1,9},{2,10},{3,11},{4,12},{5,13},{6,14},{7,15},{8,0},{9,1},... | collective-permute-start | bytes 688136 | tf_op jit(solution)/shard_map/ppermute | solution.py:61
  146.3 10.7 %collective-permute-start.32 = (bf16[128,896]{1,0:T(8,128)(2,1)S(1)}, bf16[128,896]{1,0:T(8,128)(2,1)S(1)}, u32[]{:S(2)}, u32[]{:S(2)}) collective-permute-start(bf16[128,896]{1,0:T(8,128)(2,1)S(1)} %add_convert_fusion.5), channel_id=1, source_target_pairs={{0,16},{1,17},{2,18},{3,19},{4,20},{5,21},{6,22},{7,23},{8,24},{9,... | collective-permute-start | bytes 688136 | tf_op jit(solution)/shard_map/ppermute | solution.py:61
where the time goes:
time: 158 us
  waiting for transfers between devices  79.8 us (51%)
  starting transfers between devices  37.7 us (24%)
  matrix products  28.7 us (18%)
  other arithmetic  7.04 us (4%)
  local copies, waits for them, and re-layouts  3.47 us (2%)
    ppermute x33, waiting for transfers between devices, swap(): return lax.ppermute(value, ('expert', 'mp'), pairs)  79.8 us
    ppermute x33, starting transfers between devices, swap(): return lax.ppermute(value, ('expert', 'mp'), pairs)  37.7 us
    dot_general x50, matrix products, dot(): return jnp.dot(a, b, preferred_element_type=F32)  26.5 us
  transfers between devices with their start and end apart: 33, of which 14 were waited for; matrix products, arithmetic and copies ran while one was open for 24% of the time, Pallas kernels for 0%

commit v1 on v0

v1 whole, which is shorter than its diff:
```python
import jax
import jax.numpy as jnp
from jax import lax
from jax.sharding import PartitionSpec as P


BF16 = jnp.bfloat16
F32 = jnp.float32


def bits_of(size):
    count = size.bit_length() - 1
    assert size == 1 << count
    return [1 << b for b in range(count)]


def dot(a, b):
    return jnp.dot(a, b, preferred_element_type=F32)


def three_parts(values):
    parts = []
    for _ in range(3):
        head = lax.reduce_precision(values, 8, 7)
        parts.append(head.astype(BF16))
        values = values - head
    return parts


def step(function, *values, after=()):
    held = lax.optimization_barrier(values + tuple(after))[: len(values)]
    return function(*held)


def on_device(
    tokens,
    assignments,
    gate_probs,
    expert_gate,
    expert_up,
    expert_down,
    shared_gate,
    shared_up,
    shared_down_weight,
):
    experts, parts = lax.axis_size("expert"), lax.axis_size("mp")
    expert, part = lax.axis_index("expert"), lax.axis_index("mp")
    rows, width = tokens.shape
    chosen = assignments.shape[1]
    slots = min(rows, max(2, 2 * rows * chosen // experts))
    expert_bits, part_bits = bits_of(experts), bits_of(parts)
    groups = [list(range(g, g + parts)) for g in range(0, experts, parts)]
    hidden_width = shared_gate.shape[1]

    flips = [(part & bit) != 0 for bit in part_bits]
    starts = [(part ^ j) * width for j in range(parts)]
    expert_number = expert.astype(F32)

    def swap(value, de=0, dm=0):
        pairs = [
            (e * parts + m, (e ^ de) * parts + (m ^ dm))
            for e in range(experts)
            for m in range(parts)
        ]
        return lax.ppermute(value, ("expert", "mp"), pairs)

    def by_part(values):
        values = list(values)
        for bit, flip in zip(part_bits, flips):
            values = [jnp.where(flip, values[j ^ bit], values[j]) for j in range(len(values))]
        return values

    def prepare(tokens, ids, probs):
        notes = [ids.T[k : k + 1].astype(BF16) for k in range(chosen)]
        for k in range(chosen):
            notes += three_parts(probs.T[k : k + 1])
        notes = jnp.concatenate(notes, axis=0)
        return jnp.concatenate([tokens, jnp.pad(notes, ((0, 0), (0, width - rows)))], axis=0)

    blocks = {0: step(prepare, tokens, assignments, gate_probs)}
    for bit in reversed(expert_bits[1:]):
        for k in list(blocks):
            blocks[k | bit] = swap(blocks[k], de=bit)
    for k in list(blocks):
        blocks[k | 1] = swap(blocks[k], de=1)

    slices = {0: tokens}
    for bit in part_bits[1:]:
        for j in list(slices):
            slices[j | bit] = swap(slices[j], dm=bit)
    others = [j for j in sorted(slices) if j]
    far = {0: jnp.concatenate([slices[j] for j in others], axis=1)}
    for bit in reversed(expert_bits):
        source = [k for k in sorted(far) if bit >= parts or k >= parts]
        if source:
            got = swap(jnp.stack([far[k] for k in source]), de=bit)
            for n, k in enumerate(source):
                far[k | bit] = got[n]

    before = jnp.triu(jnp.ones((rows, rows), F32), 1).astype(BF16)
    place = jnp.arange(slots, dtype=jnp.int32).astype(F32)[None, :, None]
    both = step(lambda a, b: jnp.concatenate([a, b], axis=1), shared_gate, shared_up)

    def pick(taking, *sources):
        return jnp.concatenate([dot(taking[i], b).astype(BF16) for i, b in enumerate(sources)])

    def dispatch(*members):
        table = jnp.stack([b[rows : rows + 4 * chosen, :rows] for b in members])
        ids = table[:, :chosen].astype(F32)
        probs = table[:, chosen:].astype(F32).reshape(len(members), chosen, 3, rows)
        probs = probs[:, :, 0] + (probs[:, :, 1] + probs[:, :, 2])
        mine = ids == expert_number
        named = jnp.any(mine, axis=1).astype(F32)
        rank = dot(named.astype(BF16), before)
        taking = ((rank[:, None, :] == place) & (named[:, None, :] > 0)).astype(BF16)
        row_prob = jnp.sum(jnp.where(mine, probs, 0.0), axis=1)
        return pick(taking, *[b[:rows] for b in members]), row_prob, taking

    def slot_weights(row_prob, taking):
        return jnp.sum(taking.astype(F32) * row_prob[:, None, :], axis=2)

    def shared_act(act, came):
        act = act + came.astype(F32)
        return (jax.nn.silu(act[:, :hidden_width]) * act[:, hidden_width:]).astype(BF16)

    def cut(weights, j, axis):
        at, sizes = [0, 0], list(weights.shape)
        at[axis], sizes[axis] = starts[j], width
        return lax.dynamic_slice(weights, at, sizes, allow_negative_indices=False)

    def feed(own, core):
        gate_act = up_act = 0.0
        for j in sorted(range(parts), key=lambda j: j & 1):
            rows_j = core[j // 2] if j & 1 else own[j // 2]
            gate_act += dot(rows_j, cut(expert_gate[0], j, 0))
            up_act += dot(rows_j, cut(expert_up[0], j, 0))
        return (jax.nn.silu(gate_act) * up_act).astype(BF16)

    def lower(js, kind):
        def function(hidden):
            out = []
            for j in js:
                out.append(dot(hidden, cut(expert_down[0], j, 1)).astype(kind))
            return jnp.stack(out)

        return function

    def halve(js, bit, height):
        def function(staying, came):
            go, keep = [], []
            for i, j in enumerate(js):
                span = slice(i * height, (i + 1) * height)
                value = staying[span] + came[span].astype(F32)
                (go if j & bit else keep).append(value)
            return jnp.concatenate([v.astype(BF16) for v in go]), jnp.concatenate(keep)

        return function

    odd = [j for j in range(parts) if j & 1]
    even = [j for j in range(parts) if not j & 1]
    total, routed_rows, returned, shared_hidden = {}, {}, {}, {}
    last_picked = last_act = last_left = last_weigh = ()
    for g, members in enumerate(groups):
        mine = [blocks[k] for k in members]
        routed_order = sorted(members, key=lambda k: (not k & 1, -k))
        picked, row_prob, taking = step(
            dispatch, *[blocks[k] for k in routed_order], after=last_picked
        )
        last_picked = (picked, row_prob, taking)
        weight = step(slot_weights, row_prob, taking)

        slices = {0: picked}
        if g:
            picked_far = step(pick, taking, *[far[k] for k in routed_order])
            for n, j in enumerate(others):
                slices[j] = picked_far[:, n * width : (n + 1) * width]
        else:
            for bit in part_bits[1:]:
                for j in list(slices):
                    slices[j | bit] = swap(slices[j], dm=bit)
        own = step(lambda *v: jnp.stack(v), *[slices[j] for j in even])
        core = swap(own, dm=1)

        held = step(lambda *b: tuple(by_part([x[:rows] for x in b])), *mine)

        def sums_of(js, kind):
            return lambda w, *h: dot(jnp.concatenate([h[j] for j in js]), w).astype(kind)

        leaving = step(sums_of(odd, BF16), both, *held)
        staying = step(sums_of(even, F32), both, *held)
        came = swap(leaving, dm=1)
        pending = even
        for bit in part_bits[1:]:
            leaving, staying = step(halve(pending, bit, rows), staying, came, after=last_left)
            last_left = (leaving,)
            came = swap(leaving, dm=bit)
            pending = [j for j in pending if not j & bit]
        act = step(shared_act, staying, came, after=last_act)
        last_act = (act,)

        arrays, known = [act], {0: (0, 0)}
        for bit in reversed(part_bits):
            order = sorted(known)
            got = swap(jnp.concatenate(arrays), dm=bit)
            flat = [j for i in range(len(arrays)) for j in order if known[j][0] == i]
            for n, j in enumerate(flat):
                known[j | bit] = (len(arrays), n)
            arrays.append(got)
        returned[g] = (arrays, known)

        hidden = step(feed, own, core)
        leaving = step(lower(odd, BF16), hidden)
        staying = step(lower(even, F32), hidden)
        came = swap(leaving, dm=1)
        spans = [("a", 0, 2), ("b", 1, 2)] if g == 0 else [("", 0, 1)]
        for tag, at, pieces in spans:
            height = parts * slots // pieces
            stay, got, pending = staying, came, even
            for bit in part_bits[1:]:

                def add_rows(stay, got):
                    first = height * at if stay.shape[1] > height else 0
                    span = slice(first, first + height)
                    added = [stay[i, span] + got[i, span].astype(F32) for i in range(len(pending))]
                    go = [x.astype(BF16) for x, j in zip(added, pending) if j & bit]
                    return jnp.stack(go), jnp.stack([x for x, j in zip(added, pending) if not j & bit])

                sent, stay = step(add_rows, stay, got, after=last_weigh)
                last_weigh = (sent,)
                got = swap(sent, dm=bit)
                pending = [j for j in pending if not j & bit]
            inside = slice(at * parts // pieces, (at + 1) * parts // pieces)
            order = routed_order[inside]
            routed_rows[f"{g}{tag}"] = (order, stay, got, weight, taking, inside)

    def weigh(result, came, weight):
        result = (result + came.astype(F32)).reshape(-1, slots, width)
        return (result * weight[inside][:, :, None]).astype(BF16)

    def join(hidden, result, taking):
        routed = jnp.einsum(
            "st,sd->td", taking[inside][i], result[i], preferred_element_type=F32
        )
        return dot(hidden, shared_down_weight) + routed

    last_weigh = ()
    for name in sorted(routed_rows, key=lambda n: (-int(n.rstrip("ab")), n)):
        order, here, came, weight, taking, inside = routed_rows[name]
        g = int(name.rstrip("ab"))
        if groups[g][0] not in shared_hidden:
            arrays, known = returned[g]

            def turn(*v):
                at = [known[j] for j in range(parts)]
                return tuple(by_part([v[i][n * rows : (n + 1) * rows] for i, n in at]))

            back = step(turn, *arrays, after=last_weigh)
            shared_hidden.update(zip(groups[g], back))
            last_weigh = (back[0],)
        result = step(weigh, here, came, weight, after=last_weigh)
        last_weigh = (result,)
        for i, k in enumerate(order):
            total[k] = step(join, shared_hidden[k], result, taking)

    left = list(range(experts))
    for bit in expert_bits:
        for k in sorted((k for k in left if k & bit), reverse=True):
            leaving = total[k].astype(BF16)
            came = swap(leaving, de=bit)
            total[k ^ bit] = total[k ^ bit] + came.astype(F32)
        left = [k for k in left if not k & bit]
    return total[0].astype(BF16)


def solution(mesh):
    in_specs = (
        P("expert", "mp"),
        P("expert", None),
        P("expert", None),
        P("expert", None, "mp"),
        P("expert", None, "mp"),
        P("expert", "mp", None),
        P("mp", "expert"),
        P("mp", "expert"),
        P("expert", "mp"),
    )
    out_specs = P("expert", "mp")
    return jax.shard_map(
        on_device, mesh=mesh, in_specs=in_specs, out_specs=out_specs, check_vma=False
    )
```

time: 158 us -> 167 us (1.057)
  waiting for transfers between devices: 79.8 us -> 95 us
  starting transfers between devices: 37.7 us -> 31.5 us
    ppermute x33 -> x34, waiting for transfers between devices: 79.8 us -> 95 us  [swap(): return lax.ppermute(value, ('expert', 'mp'), pairs)]
    ppermute x33 -> x34, starting transfers between devices: 37.7 us -> 31.5 us  [swap(): return lax.ppermute(value, ('expert', 'mp'), pairs)]
  transfers between devices with their start and end apart: 33 -> 34, of which waited for: 14 -> 15; matrix products, arithmetic and copies ran while one was open for 24% -> 21% of each run, Pallas kernels for 0% -> 0%
where the time goes in v1:
time: 167 us; the launch traced here: 166 us
  waiting for transfers between devices  95 us (57%)
  starting transfers between devices  31.5 us (19%)
  matrix products  28.5 us (17%)
  other arithmetic  7.55 us (5%)
  local copies, waits for them, and re-layouts  2.89 us (2%)
    ppermute x34, waiting for transfers between devices, swap(): return lax.ppermute(value, ('expert', 'mp'), pairs)  95 us
    ppermute x34, starting transfers between devices, swap(): return lax.ppermute(value, ('expert', 'mp'), pairs)  31.5 us
    dot_general x50, matrix products, dot(): return jnp.dot(a, b, preferred_element_type=F32)  26.5 us
  transfers between devices with their start and end apart: 34, of which 15 were waited for; matrix products, arithmetic and copies ran while one was open for 21% of the time, Pallas kernels for 0%

profile of v1, /device:TPU:0, one launch (start us, length us, event | category | flops | bytes accessed | tf_op | source)
XLA Modules:
  0.0 166.5 jit_solution(5872900070907125874)
XLA Ops:
  0.0 0.9 fusion.211
  0.9 0.7 convert_bitcast_fusion
  1.6 1.0 fusion.113
  2.5 3.1 %collective-permute-start.1 = (bf16[136,896]{1,0:T(8,128)(2,1)S(1)}, bf16[136,896]{1,0:T(8,128)(2,1)S(1)}, u32[]{:S(2)}, u32[]{:S(2)}) collective-permute-start(bf16[136,896]{1,0:T(8,128)(2,1)S(1)} %fusion.113), channel_id=1, source_target_pairs={{0,8},{1,9},{2,10},{3,11},{4,12},{5,13},{6,14},{7,15},{8,0},{9,1},... | collective-permute-start | bytes 731144 | tf_op jit(solution)/shard_map/ppermute | solution.py:65
  5.7 1.5 collective-permute-start
  7.2 2.6 %collective-permute-start.7 = (bf16[136,896]{1,0:T(8,128)(2,1)S(1)}, bf16[136,896]{1,0:T(8,128)(2,1)S(1)}, u32[]{:S(2)}, u32[]{:S(2)}) collective-permute-start(bf16[136,896]{1,0:T(8,128)(2,1)S(1)} %fusion.113), channel_id=1, source_target_pairs={{0,16},{1,17},{2,18},{3,19},{4,20},{5,21},{6,22},{7,23},{8,24},{9,... | collective-permute-start | bytes 731144 | tf_op jit(solution)/shard_map/ppermute | solution.py:65
  9.8 1.5 collective-permute-start.11
  11.3 2.0 %constant_dynamic-update-slice_fusion.1 = bf16[896,2560]{1,0:T(8,128)(2,1)S(1)} fusion(bf16[896,1280]{1,0:T(8,128)(2,1)} %param.15), kind=kLoop, calls=%fused_computation.304 | loop fusion | bytes 4587520
  13.2 3.2 %collective-permute-done.11 = bf16[128,896]{1,0:T(8,128)(2,1)S(1)} collective-permute-done((bf16[128,896]{1,0:T(8,128)(2,1)}, bf16[128,896]{1,0:T(8,128)(2,1)S(1)}, u32[]{:S(2)}, u32[]{:S(2)}) %collective-permute-start.11) | collective-permute-done | bytes 229408 | tf_op jit(solution)/shard_map/ppermute | solution.py:65
  16.8 1.3 collective-permute-start.2
  18.3 8.5 %collective-permute-done.7 = bf16[136,896]{1,0:T(8,128)(2,1)S(1)} collective-permute-done((bf16[136,896]{1,0:T(8,128)(2,1)S(1)}, bf16[136,896]{1,0:T(8,128)(2,1)S(1)}, u32[]{:S(2)}, u32[]{:S(2)}) %collective-permute-start.7) | collective-permute-done | bytes 243744 | tf_op jit(solution)/shard_map/ppermute | solution.py:65
  27.0 3.4 %collective-permute-done.12 = bf16[1,128,896]{2,1,0:T(8,128)(2,1)S(1)} collective-permute-done((bf16[1,128,896]{2,1,0:T(8,128)(2,1)S(1)}, bf16[1,128,896]{2,1,0:T(8,128)(2,1)S(1)}, u32[]{:S(2)}, u32[]{:S(2)}) %collective-permute-start.12) | collective-permute-done | bytes 229408 | tf_op jit(solution)/shard_map/ppermute | solution.py:65
  31.5 1.6 collective-permute-start.17
  33.2 1.5 convolution_convert_fusion.1
  34.8 0.8 collective-permute-done.8
  35.6 1.5 fusion.67
  37.2 3.2 %collective-permute-done.13 = bf16[1,128,896]{2,1,0:T(8,128)(2,1)S(1)} collective-permute-done((bf16[1,128,896]{2,1,0:T(8,128)(2,1)S(1)}, bf16[1,128,896]{2,1,0:T(8,128)(2,1)S(1)}, u32[]{:S(2)}, u32[]{:S(2)}) %collective-permute-start.13) | collective-permute-done | bytes 229408 | tf_op jit(solution)/shard_map/ppermute | solution.py:65
  40.5 3.0 %collective-permute-done.9 = bf16[136,896]{1,0:T(8,128)(2,1)S(1)} collective-permute-done((bf16[136,896]{1,0:T(8,128)(2,1)S(1)}, bf16[136,896]{1,0:T(8,128)(2,1)S(1)}, u32[]{:S(2)}, u32[]{:S(2)}) %collective-permute-start.9) | collective-permute-done | bytes 243744 | tf_op jit(solution)/shard_map/ppermute | solution.py:65
  44.7 1.5 convolution_convert_fusion
  46.5 1.5 fusion.74
  48.1 0.6 collective-permute-start.18
  48.7 4.5 %collective-permute-done.14 = bf16[2,128,896]{2,1,0:T(8,128)(2,1)S(1)} collective-permute-done((bf16[2,128,896]{2,1,0:T(8,128)(2,1)S(1)}, bf16[2,128,896]{2,1,0:T(8,128)(2,1)S(1)}, u32[]{:S(2)}, u32[]{:S(2)}) %collective-permute-start.14) | collective-permute-done | bytes 458784 | tf_op jit(solution)/shard_map/ppermute | solution.py:65
  54.5 1.6 collective-permute-start.4
  56.0 0.6 fusion.36
  56.6 0.6 fusion.26
  57.2 0.6 convolution_add_fusion.5
  57.8 0.6 convolution_add_fusion.2
  58.4 0.6 convolution_add_fusion.4
  59.0 0.6 convolution_add_fusion.1
  59.6 0.6 convolution_add_fusion.3
  60.1 0.6 fusion.3
  61.9 0.8 fusion.7
  63.6 0.6 convolution_bitcast_fusion
  64.6 1.1 collective-permute-start.22
  65.7 0.6 fusion.38
  66.2 0.6 fusion.28
  66.8 0.6 convolution_add_fusion.11
  67.4 0.6 convolution_add_fusion.10
  68.0 0.6 convolution_add_fusion.9
  68.5 0.6 convolution_add_fusion.8
  69.1 0.6 convolution_add_fusion.7
  69.7 0.6 fusion.2
  70.3 0.6 fusion.4
  70.8 0.6 fusion.5
  72.4 0.6 convolution_bitcast_fusion.2
  73.3 12.4 %collective-permute-done.22 = bf16[128,2560]{1,0:T(8,128)(2,1)S(1)} collective-permute-done((bf16[128,2560]{1,0:T(8,128)(2,1)S(1)}, bf16[128,2560]{1,0:T(8,128)(2,1)S(1)}, u32[]{:S(2)}, u32[]{:S(2)}) %collective-permute-start.22) | collective-permute-done | bytes 655392 | tf_op jit(solution)/shard_map/ppermute | solution.py:65
  86.1 1.6 collective-permute-start.23
  87.8 0.6 collective-permute-start.5
  88.5 1.6 collective-permute-start.26
  90.1 6.6 %collective-permute-done.23 = bf16[128,1280]{1,0:T(8,128)(2,1)S(1)} collective-permute-done((bf16[128,1280]{1,0:T(8,128)(2,1)S(1)}, bf16[128,1280]{1,0:T(8,128)(2,1)S(1)}, u32[]{:S(2)}, u32[]{:S(2)}) %collective-permute-start.23) | collective-permute-done | bytes 327712 | tf_op jit(solution)/shard_map/ppermute | solution.py:65
  96.8 6.9 %collective-permute-done.5 = bf16[128,1280]{1,0:T(8,128)(2,1)S(1)} collective-permute-done((bf16[128,1280]{1,0:T(8,128)(2,1)S(1)}, bf16[128,1280]{1,0:T(8,128)(2,1)S(1)}, u32[]{:S(2)}, u32[]{:S(2)}) %collective-permute-start.5) | collective-permute-done | bytes 327712 | tf_op jit(solution)/shard_map/ppermute | solution.py:65
  103.9 1.6 collective-permute-start.25
  105.7 0.6 collective-permute-start.20
  106.5 15.6 %collective-permute-done.20 = bf16[1,256,896]{2,1,0:T(8,128)(2,1)S(1)} collective-permute-done((bf16[1,256,896]{2,1,0:T(8,128)(2,1)S(1)}, bf16[1,256,896]{2,1,0:T(8,128)(2,1)S(1)}, u32[]{:S(2)}, u32[]{:S(2)}) %collective-permute-start.20) | collective-permute-done | bytes 458784 | tf_op jit(solution)/shard_map/ppermute | solution.py:65
  125.8 1.8 %collective-permute-start.28 = (bf16[128,896]{1,0:T(8,128)(2,1)S(1)}, bf16[128,896]{1,0:T(8,128)(2,1)S(1)}, u32[]{:S(2)}, u32[]{:S(2)}) collective-permute-start(bf16[128,896]{1,0:T(8,128)(2,1)S(1)} %fusion.9), channel_id=1, source_target_pairs={{0,4},{1,5},{2,6},{3,7},{4,0},{5,1},{6,2},{7,3},{8,12},{9,13},{10,... | collective-permute-start | bytes 688136 | tf_op jit(solution)/shard_map/ppermute | solution.py:65
  127.6 0.8 fusion.229
  130.8 1.8 %collective-permute-start.31 = (bf16[128,896]{1,0:T(8,128)(2,1)S(1)}, bf16[128,896]{1,0:T(8,128)(2,1)S(1)}, u32[]{:S(2)}, u32[]{:S(2)}) collective-permute-start(bf16[128,896]{1,0:T(8,128)(2,1)S(1)} %fusion.11), channel_id=1, source_target_pairs={{0,4},{1,5},{2,6},{3,7},{4,0},{5,1},{6,2},{7,3},{8,12},{9,13},{10,... | collective-permute-start | bytes 688136 | tf_op jit(solution)/shard_map/ppermute | solution.py:65
  132.8 12.8 %collective-permute-done.31 = bf16[128,896]{1,0:T(8,128)(2,1)S(1)} collective-permute-done((bf16[128,896]{1,0:T(8,128)(2,1)S(1)}, bf16[128,896]{1,0:T(8,128)(2,1)S(1)}, u32[]{:S(2)}, u32[]{:S(2)}) %collective-permute-start.31) | collective-permute-done | bytes 229408 | tf_op jit(solution)/shard_map/ppermute | solution.py:65
  145.8 1.9 %collective-permute-start.32 = (bf16[128,896]{1,0:T(8,128)(2,1)S(1)}, bf16[128,896]{1,0:T(8,128)(2,1)S(1)}, u32[]{:S(2)}, u32[]{:S(2)}) collective-permute-start(bf16[128,896]{1,0:T(8,128)(2,1)S(1)} %add_convert_fusion.5), channel_id=1, source_target_pairs={{0,8},{1,9},{2,10},{3,11},{4,12},{5,13},{6,14},{7,15},{8,0},{9,1},... | collective-permute-start | bytes 688136 | tf_op jit(solution)/shard_map/ppermute | solution.py:65
  148.2 6.1 %collective-permute-done.32 = bf16[128,896]{1,0:T(8,128)(2,1)S(1)} collective-permute-done((bf16[128,896]{1,0:T(8,128)(2,1)S(1)}, bf16[128,896]{1,0:T(8,128)(2,1)S(1)}, u32[]{:S(2)}, u32[]{:S(2)}) %collective-permute-start.32) | collective-permute-done | bytes 229408 | tf_op jit(solution)/shard_map/ppermute | solution.py:65
  154.5 2.9 %collective-permute-start.33 = (bf16[128,896]{1,0:T(8,128)(2,1)S(1)}, bf16[128,896]{1,0:T(8,128)(2,1)S(1)}, u32[]{:S(2)}, u32[]{:S(2)}) collective-permute-start(bf16[128,896]{1,0:T(8,128)(2,1)S(1)} %add_convert_fusion.4), channel_id=1, source_target_pairs={{0,16},{1,17},{2,18},{3,19},{4,20},{5,21},{6,22},{7,23},{8,24},{9,... | collective-permute-start | bytes 688136 | tf_op jit(solution)/shard_map/ppermute | solution.py:65
  157.6 3.1 %collective-permute-done.29 = bf16[128,896]{1,0:T(8,128)(2,1)S(1)} collective-permute-done((bf16[128,896]{1,0:T(8,128)(2,1)S(1)}, bf16[128,896]{1,0:T(8,128)(2,1)S(1)}, u32[]{:S(2)}, u32[]{:S(2)}) %collective-permute-start.29) | collective-permute-done | bytes 229408 | tf_op jit(solution)/shard_map/ppermute | solution.py:65
  160.7 5.0 %collective-permute-done.33 = bf16[128,896]{1,0:T(8,128)(2,1)S(1)} collective-permute-done((bf16[128,896]{1,0:T(8,128)(2,1)S(1)}, bf16[128,896]{1,0:T(8,128)(2,1)S(1)}, u32[]{:S(2)}, u32[]{:S(2)}) %collective-permute-start.33) | collective-permute-done | bytes 229408 | tf_op jit(solution)/shard_map/ppermute | solution.py:65
  165.7 0.8 add_convert_fusion.3
  (146 shorter events, 17.3 us)
Async XLA Ops:
  0.0 122.6 %copy-start = (bf16[1280,896]{1,0:T(8,128)(2,1)S(1)}, bf16[1280,896]{1,0:T(8,128)(2,1)}, u32[]{:S(2)}) copy-start(bf16[1280,896]{1,0:T(8,128)(2,1)} %param.17) | copy-start | bytes 6881284
  2.5 14.3 %collective-permute-start.1 = (bf16[136,896]{1,0:T(8,128)(2,1)S(1)}, bf16[136,896]{1,0:T(8,128)(2,1)S(1)}, u32[]{:S(2)}, u32[]{:S(2)}) collective-permute-start(bf16[136,896]{1,0:T(8,128)(2,1)S(1)} %fusion.113), channel_id=1, source_target_pairs={{0,8},{1,9},{2,10},{3,11},{4,12},{5,13},{6,14},{7,15},{8,0},{9,1},... | collective-permute-start | bytes 731144 | tf_op jit(solution)/shard_map/ppermute | solution.py:65
  5.7 24.7 %collective-permute-start = (bf16[136,896]{1,0:T(8,128)(2,1)S(1)}, bf16[136,896]{1,0:T(8,128)(2,1)S(1)}, u32[]{:S(2)}, u32[]{:S(2)}) collective-permute-start(bf16[136,896]{1,0:T(8,128)(2,1)S(1)} %fusion.113), channel_id=1, source_target_pairs={{0,4},{1,5},{2,6},{3,7},{4,0},{5,1},{6,2},{7,3},{8,12},{9,13},{10,... | collective-permute-start | bytes 731144 | tf_op jit(solution)/shard_map/ppermute | solution.py:65
  7.2 19.6 %collective-permute-start.7 = (bf16[136,896]{1,0:T(8,128)(2,1)S(1)}, bf16[136,896]{1,0:T(8,128)(2,1)S(1)}, u32[]{:S(2)}, u32[]{:S(2)}) collective-permute-start(bf16[136,896]{1,0:T(8,128)(2,1)S(1)} %fusion.113), channel_id=1, source_target_pairs={{0,16},{1,17},{2,18},{3,19},{4,20},{5,21},{6,22},{7,23},{8,24},{9,... | collective-permute-start | bytes 731144 | tf_op jit(solution)/shard_map/ppermute | solution.py:65
  9.8 6.7 %collective-permute-start.11 = (bf16[128,896]{1,0:T(8,128)(2,1)}, bf16[128,896]{1,0:T(8,128)(2,1)S(1)}, u32[]{:S(2)}, u32[]{:S(2)}) collective-permute-start(bf16[128,896]{1,0:T(8,128)(2,1)} %param.9), channel_id=1, source_target_pairs={{0,2},{1,3},{2,0},{3,1},{4,6},{5,7},{6,4},{7,5},{8,10},{9,11},{10,... | collective-permute-start | bytes 688136 | tf_op jit(solution)/shard_map/ppermute | solution.py:65
  11.3 6.9 %copy-start.1 = (bf16[896,1280]{1,0:T(8,128)(2,1)S(1)}, bf16[896,1280]{1,0:T(8,128)(2,1)}, u32[]{:S(2)}) copy-start(bf16[896,1280]{1,0:T(8,128)(2,1)} %param.16) | copy-start | bytes 6881284
  16.5 13.9 %collective-permute-start.12 = (bf16[1,128,896]{2,1,0:T(8,128)(2,1)S(1)}, bf16[1,128,896]{2,1,0:T(8,128)(2,1)S(1)}, u32[]{:S(2)}, u32[]{:S(2)}) collective-permute-start(bf16[1,128,896]{2,1,0:T(8,128)(2,1)S(1)} %bitcast.301), channel_id=1, source_target_pairs={{0,16},{1,17},{2,18},{3,19},{4,20},{5,21},{6,22},{7,23},{8,24},{9,... | collective-permute-start | bytes 688136 | tf_op jit(solution)/shard_map/ppermute | solution.py:65
  16.8 13.6 %collective-permute-start.2 = (bf16[136,896]{1,0:T(8,128)(2,1)S(1)}, bf16[136,896]{1,0:T(8,128)(2,1)S(1)}, u32[]{:S(2)}, u32[]{:S(2)}) collective-permute-start(bf16[136,896]{1,0:T(8,128)(2,1)S(1)} %collective-permute-done.1), channel_id=1, source_target_pairs={{0,4},{1,5},{2,6},{3,7},{4,0},{5,1},{6,2},{7,3},{8,12},{9,13},{10,... | collective-permute-start | bytes 731144 | tf_op jit(solution)/shard_map/ppermute | solution.py:65
  26.8 8.8 %collective-permute-start.8 = (bf16[136,896]{1,0:T(8,128)(2,1)S(1)}, bf16[136,896]{1,0:T(8,128)(2,1)S(1)}, u32[]{:S(2)}, u32[]{:S(2)}) collective-permute-start(bf16[136,896]{1,0:T(8,128)(2,1)S(1)} %collective-permute-done.7), channel_id=1, source_target_pairs={{0,8},{1,9},{2,10},{3,11},{4,12},{5,13},{6,14},{7,15},{8,0},{9,1},... | collective-permute-start | bytes 731144 | tf_op jit(solution)/shard_map/ppermute | solution.py:65
  26.8 13.7 %collective-permute-start.10 = (bf16[136,896]{1,0:T(8,128)(2,1)S(1)}, bf16[136,896]{1,0:T(8,128)(2,1)S(1)}, u32[]{:S(2)}, u32[]{:S(2)}) collective-permute-start(bf16[136,896]{1,0:T(8,128)(2,1)S(1)} %collective-permute-done.7), channel_id=1, source_target_pairs={{0,4},{1,5},{2,6},{3,7},{4,0},{5,1},{6,2},{7,3},{8,12},{9,13},{10,... | collective-permute-start | bytes 731144 | tf_op jit(solution)/shard_map/ppermute | solution.py:65
  30.4 10.0 %collective-permute-start.13 = (bf16[1,128,896]{2,1,0:T(8,128)(2,1)S(1)}, bf16[1,128,896]{2,1,0:T(8,128)(2,1)S(1)}, u32[]{:S(2)}, u32[]{:S(2)}) collective-permute-start(bf16[1,128,896]{2,1,0:T(8,128)(2,1)S(1)} %collective-permute-done.12), channel_id=1, source_target_pairs={{0,8},{1,9},{2,10},{3,11},{4,12},{5,13},{6,14},{7,15},{8,0},{9,1},... | collective-permute-start | bytes 688136 | tf_op jit(solution)/shard_map/ppermute | solution.py:65
  31.5 16.5 %collective-permute-start.17 = (bf16[256,896]{1,0:T(8,128)(2,1)S(1)}, bf16[256,896]{1,0:T(8,128)(2,1)S(1)}, u32[]{:S(2)}, u32[]{:S(2)}) collective-permute-start(bf16[256,896]{1,0:T(8,128)(2,1)S(1)} %pad_maximum_fusion.8), channel_id=1, source_target_pairs={{0,2},{1,3},{2,0},{3,1},{4,6},{5,7},{6,4},{7,5},{8,10},{9,11},{10,... | collective-permute-start | bytes 1376264 | tf_op jit(solution)/shard_map/ppermute | solution.py:65
  34.7 19.4 %collective-permute-start.3 = (bf16[256,2560]{1,0:T(8,128)(2,1)S(1)}, bf16[256,2560]{1,0:T(8,128)(2,1)S(1)}, u32[]{:S(2)}, u32[]{:S(2)}) collective-permute-start(bf16[256,2560]{1,0:T(8,128)(2,1)S(1)} %convolution_convert_fusion.1), channel_id=1, source_target_pairs={{0,1},{1,0},{2,3},{3,2},{4,5},{5,4},{6,7},{7,6},{8,9},{9,8},{10,11... | collective-permute-start | bytes 3932168 | tf_op jit(solution)/shard_map/ppermute | solution.py:65
  35.6 7.9 %collective-permute-start.9 = (bf16[136,896]{1,0:T(8,128)(2,1)S(1)}, bf16[136,896]{1,0:T(8,128)(2,1)S(1)}, u32[]{:S(2)}, u32[]{:S(2)}) collective-permute-start(bf16[136,896]{1,0:T(8,128)(2,1)S(1)} %collective-permute-done.8), channel_id=1, source_target_pairs={{0,4},{1,5},{2,6},{3,7},{4,0},{5,1},{6,2},{7,3},{8,12},{9,13},{10,... | collective-permute-start | bytes 731144 | tf_op jit(solution)/shard_map/ppermute | solution.py:65
  40.5 12.7 %collective-permute-start.14 = (bf16[2,128,896]{2,1,0:T(8,128)(2,1)S(1)}, bf16[2,128,896]{2,1,0:T(8,128)(2,1)S(1)}, u32[]{:S(2)}, u32[]{:S(2)}) collective-permute-start(bf16[2,128,896]{2,1,0:T(8,128)(2,1)S(1)} %pad_maximum_fusion.10), channel_id=1, source_target_pairs={{0,4},{1,5},{2,6},{3,7},{4,0},{5,1},{6,2},{7,3},{8,12},{9,13},{10,... | collective-permute-start | bytes 1376264 | tf_op jit(solution)/shard_map/ppermute | solution.py:65
  46.2 18.1 %collective-permute-start.21 = (bf16[256,2560]{1,0:T(8,128)(2,1)S(1)}, bf16[256,2560]{1,0:T(8,128)(2,1)S(1)}, u32[]{:S(2)}, u32[]{:S(2)}) collective-permute-start(bf16[256,2560]{1,0:T(8,128)(2,1)S(1)} %convolution_convert_fusion), channel_id=1, source_target_pairs={{0,1},{1,0},{2,3},{3,2},{4,5},{5,4},{6,7},{7,6},{8,9},{9,8},{10,11... | collective-permute-start | bytes 3932168 | tf_op jit(solution)/shard_map/ppermute | solution.py:65
  48.0 8.0 %slice-start = ((s8[4587520]{0:T(1024)(128)(4,1)}), s8[4194304]{0:T(1024)(128)(4,1)S(1)}, s32[]{:S(2)}) async-start(s8[4587520]{0:T(1024)(128)(4,1)} %bitcast.283), calls=%async_computation | async-start | bytes 8388608
  48.1 7.9 %collective-permute-start.18 = (bf16[2,256,896]{2,1,0:T(8,128)(2,1)S(1)}, bf16[2,256,896]{2,1,0:T(8,128)(2,1)S(1)}, u32[]{:S(2)}, u32[]{:S(2)}) collective-permute-start(bf16[2,256,896]{2,1,0:T(8,128)(2,1)S(1)} %pad_maximum_fusion.4), channel_id=1, source_target_pairs={{0,1},{1,0},{2,3},{3,2},{4,5},{5,4},{6,7},{7,6},{8,9},{9,8},{10,11... | collective-permute-start | bytes 2752520 | tf_op jit(solution)/shard_map/ppermute | solution.py:65
  54.0 2.1 %slice-start.1 = ((s8[4587520]{0:T(1024)(128)(4,1)}), s8[393216]{0:T(1024)(128)(4,1)S(1)}, s32[]{:S(2)}) async-start(s8[4587520]{0:T(1024)(128)(4,1)} %bitcast.283), calls=%async_computation.1 | async-start | bytes 786432
  54.0 2.6 %slice-start.4 = ((s8[4587520]{0:T(1024)(128)(4,1)}), s8[4194304]{0:T(1024)(128)(4,1)S(1)}, s32[]{:S(2)}) async-start(s8[4587520]{0:T(1024)(128)(4,1)} %bitcast.287), calls=%async_computation.4 | async-start | bytes 8388608
  54.1 2.5 %slice-start.5 = ((s8[4587520]{0:T(1024)(128)(4,1)}), s8[393216]{0:T(1024)(128)(4,1)S(1)}, s32[]{:S(2)}) async-start(s8[4587520]{0:T(1024)(128)(4,1)} %bitcast.287), calls=%async_computation.5 | async-start | bytes 786432
  54.1 11.6 %collective-permute-start.15 = (bf16[2,256,896]{2,1,0:T(8,128)(2,1)S(1)}, bf16[2,256,896]{2,1,0:T(8,128)(2,1)S(1)}, u32[]{:S(2)}, u32[]{:S(2)}) collective-permute-start(bf16[2,256,896]{2,1,0:T(8,128)(2,1)S(1)} %pad_maximum_fusion.2), channel_id=1, source_target_pairs={{0,1},{1,0},{2,3},{3,2},{4,5},{5,4},{6,7},{7,6},{8,9},{9,8},{10,11... | collective-permute-start | bytes 2752520 | tf_op jit(solution)/shard_map/ppermute | solution.py:65
  54.5 18.5 %collective-permute-start.4 = (bf16[128,2560]{1,0:T(8,128)(2,1)S(1)}, bf16[128,2560]{1,0:T(8,128)(2,1)S(1)}, u32[]{:S(2)}, u32[]{:S(2)}) collective-permute-start(bf16[128,2560]{1,0:T(8,128)(2,1)S(1)} %get-tuple-element.212), channel_id=1, source_target_pairs={{0,2},{1,3},{2,0},{3,1},{4,6},{5,7},{6,4},{7,5},{8,10},{9,11},{10,... | collective-permute-start | bytes 1966088 | tf_op jit(solution)/shard_map/ppermute | solution.py:65
  59.0 2.2 %slice-start.2 = ((s8[4587520]{0:T(1024)(128)(4,1)}), s8[4194304]{0:T(1024)(128)(4,1)S(1)}, s32[]{:S(2)}) async-start(s8[4587520]{0:T(1024)(128)(4,1)} %bitcast.285), calls=%async_computation.2 | async-start | bytes 8388608
  59.5 1.8 %slice-start.3 = ((s8[4587520]{0:T(1024)(128)(4,1)}), s8[393216]{0:T(1024)(128)(4,1)S(1)}, s32[]{:S(2)}) async-start(s8[4587520]{0:T(1024)(128)(4,1)} %bitcast.285), calls=%async_computation.3 | async-start | bytes 786432
  62.8 25.7 %collective-permute-start.19 = (bf16[2,256,896]{2,1,0:T(8,128)(2,1)S(1)}, bf16[2,256,896]{2,1,0:T(8,128)(2,1)S(1)}, u32[]{:S(2)}, u32[]{:S(2)}) collective-permute-start(bf16[2,256,896]{2,1,0:T(8,128)(2,1)S(1)} %pad_maximum_fusion.5), channel_id=1, source_target_pairs={{0,1},{1,0},{2,3},{3,2},{4,5},{5,4},{6,7},{7,6},{8,9},{9,8},{10,11... | collective-permute-start | bytes 2752520 | tf_op jit(solution)/shard_map/ppermute | solution.py:65
  64.6 21.1 %collective-permute-start.22 = (bf16[128,2560]{1,0:T(8,128)(2,1)S(1)}, bf16[128,2560]{1,0:T(8,128)(2,1)S(1)}, u32[]{:S(2)}, u32[]{:S(2)}) collective-permute-start(bf16[128,2560]{1,0:T(8,128)(2,1)S(1)} %get-tuple-element.213), channel_id=1, source_target_pairs={{0,2},{1,3},{2,0},{3,1},{4,6},{5,7},{6,4},{7,5},{8,10},{9,11},{10,... | collective-permute-start | bytes 1966088 | tf_op jit(solution)/shard_map/ppermute | solution.py:65
  71.5 34.0 %collective-permute-start.16 = (bf16[2,256,896]{2,1,0:T(8,128)(2,1)S(1)}, bf16[2,256,896]{2,1,0:T(8,128)(2,1)S(1)}, u32[]{:S(2)}, u32[]{:S(2)}) collective-permute-start(bf16[2,256,896]{2,1,0:T(8,128)(2,1)S(1)} %pad_maximum_fusion.3), channel_id=1, source_target_pairs={{0,1},{1,0},{2,3},{3,2},{4,5},{5,4},{6,7},{7,6},{8,9},{9,8},{10,11... | collective-permute-start | bytes 2752520 | tf_op jit(solution)/shard_map/ppermute | solution.py:65
  86.1 10.6 %collective-permute-start.23 = (bf16[128,1280]{1,0:T(8,128)(2,1)S(1)}, bf16[128,1280]{1,0:T(8,128)(2,1)S(1)}, u32[]{:S(2)}, u32[]{:S(2)}) collective-permute-start(bf16[128,1280]{1,0:T(8,128)(2,1)S(1)} %fusion.64), channel_id=1, source_target_pairs={{0,2},{1,3},{2,0},{3,1},{4,6},{5,7},{6,4},{7,5},{8,10},{9,11},{10,... | collective-permute-start | bytes 983048 | tf_op jit(solution)/shard_map/ppermute | solution.py:65
  87.8 15.9 %collective-permute-start.5 = (bf16[128,1280]{1,0:T(8,128)(2,1)S(1)}, bf16[128,1280]{1,0:T(8,128)(2,1)S(1)}, u32[]{:S(2)}, u32[]{:S(2)}) collective-permute-start(bf16[128,1280]{1,0:T(8,128)(2,1)S(1)} %fusion.65), channel_id=1, source_target_pairs={{0,2},{1,3},{2,0},{3,1},{4,6},{5,7},{6,4},{7,5},{8,10},{9,11},{10,... | collective-permute-start | bytes 983048 | tf_op jit(solution)/shard_map/ppermute | solution.py:65
  88.5 33.9 %collective-permute-start.26 = (bf16[1,128,896]{2,1,0:T(8,128)(2,1)S(1)}, bf16[1,128,896]{2,1,0:T(8,128)(2,1)S(1)}, u32[]{:S(2)}, u32[]{:S(2)}) collective-permute-start(bf16[1,128,896]{2,1,0:T(8,128)(2,1)S(1)} %get-tuple-element.218), channel_id=1, source_target_pairs={{0,2},{1,3},{2,0},{3,1},{4,6},{5,7},{6,4},{7,5},{8,10},{9,11},{10,... | collective-permute-start | bytes 688136 | tf_op jit(solution)/shard_map/ppermute | solution.py:65
  96.8 9.6 %collective-permute-start.24 = (bf16[256,1280]{1,0:T(8,128)(2,1)S(1)}, bf16[256,1280]{1,0:T(8,128)(2,1)S(1)}, u32[]{:S(2)}, u32[]{:S(2)}) collective-permute-start(bf16[256,1280]{1,0:T(8,128)(2,1)S(1)} %pad_maximum_fusion.7), channel_id=1, source_target_pairs={{0,1},{1,0},{2,3},{3,2},{4,5},{5,4},{6,7},{7,6},{8,9},{9,8},{10,11... | collective-permute-start | bytes 1966088 | tf_op jit(solution)/shard_map/ppermute | solution.py:65
  103.8 18.5 %collective-permute-start.6 = (bf16[256,1280]{1,0:T(8,128)(2,1)S(1)}, bf16[256,1280]{1,0:T(8,128)(2,1)S(1)}, u32[]{:S(2)}, u32[]{:S(2)}) collective-permute-start(bf16[256,1280]{1,0:T(8,128)(2,1)S(1)} %pad_maximum_fusion.6), channel_id=1, source_target_pairs={{0,1},{1,0},{2,3},{3,2},{4,5},{5,4},{6,7},{7,6},{8,9},{9,8},{10,11... | collective-permute-start | bytes 1966088 | tf_op jit(solution)/shard_map/ppermute | solution.py:65
  103.9 19.9 %collective-permute-start.25 = (bf16[1,128,896]{2,1,0:T(8,128)(2,1)S(1)}, bf16[1,128,896]{2,1,0:T(8,128)(2,1)S(1)}, u32[]{:S(2)}, u32[]{:S(2)}) collective-permute-start(bf16[1,128,896]{2,1,0:T(8,128)(2,1)S(1)} %get-tuple-element.216), channel_id=1, source_target_pairs={{0,2},{1,3},{2,0},{3,1},{4,6},{5,7},{6,4},{7,5},{8,10},{9,11},{10,... | collective-permute-start | bytes 688136 | tf_op jit(solution)/shard_map/ppermute | solution.py:65
  105.7 16.3 %collective-permute-start.20 = (bf16[1,256,896]{2,1,0:T(8,128)(2,1)S(1)}, bf16[1,256,896]{2,1,0:T(8,128)(2,1)S(1)}, u32[]{:S(2)}, u32[]{:S(2)}) collective-permute-start(bf16[1,256,896]{2,1,0:T(8,128)(2,1)S(1)} %get-tuple-element.219), channel_id=1, source_target_pairs={{0,2},{1,3},{2,0},{3,1},{4,6},{5,7},{6,4},{7,5},{8,10},{9,11},{10,... | collective-permute-start | bytes 1376264 | tf_op jit(solution)/shard_map/ppermute | solution.py:65
  123.4 34.2 %collective-permute-start.27 = (bf16[128,896]{1,0:T(8,128)(2,1)S(1)}, bf16[128,896]{1,0:T(8,128)(2,1)S(1)}, u32[]{:S(2)}, u32[]{:S(2)}) collective-permute-start(bf16[128,896]{1,0:T(8,128)(2,1)S(1)} %fusion.8), channel_id=1, source_target_pairs={{0,4},{1,5},{2,6},{3,7},{4,0},{5,1},{6,2},{7,3},{8,12},{9,13},{10,... | collective-permute-start | bytes 688136 | tf_op jit(solution)/shard_map/ppermute | solution.py:65
  125.8 22.0 %collective-permute-start.28 = (bf16[128,896]{1,0:T(8,128)(2,1)S(1)}, bf16[128,896]{1,0:T(8,128)(2,1)S(1)}, u32[]{:S(2)}, u32[]{:S(2)}) collective-permute-start(bf16[128,896]{1,0:T(8,128)(2,1)S(1)} %fusion.9), channel_id=1, source_target_pairs={{0,4},{1,5},{2,6},{3,7},{4,0},{5,1},{6,2},{7,3},{8,12},{9,13},{10,... | collective-permute-start | bytes 688136 | tf_op jit(solution)/shard_map/ppermute | solution.py:65
  128.6 19.7 %collective-permute-start.30 = (bf16[128,896]{1,0:T(8,128)(2,1)S(1)}, bf16[128,896]{1,0:T(8,128)(2,1)S(1)}, u32[]{:S(2)}, u32[]{:S(2)}) collective-permute-start(bf16[128,896]{1,0:T(8,128)(2,1)S(1)} %fusion.10), channel_id=1, source_target_pairs={{0,4},{1,5},{2,6},{3,7},{4,0},{5,1},{6,2},{7,3},{8,12},{9,13},{10,... | collective-permute-start | bytes 688136 | tf_op jit(solution)/shard_map/ppermute | solution.py:65
  130.8 14.8 %collective-permute-start.31 = (bf16[128,896]{1,0:T(8,128)(2,1)S(1)}, bf16[128,896]{1,0:T(8,128)(2,1)S(1)}, u32[]{:S(2)}, u32[]{:S(2)}) collective-permute-start(bf16[128,896]{1,0:T(8,128)(2,1)S(1)} %fusion.11), channel_id=1, source_target_pairs={{0,4},{1,5},{2,6},{3,7},{4,0},{5,1},{6,2},{7,3},{8,12},{9,13},{10,... | collective-permute-start | bytes 688136 | tf_op jit(solution)/shard_map/ppermute | solution.py:65
  145.8 8.6 %collective-permute-start.32 = (bf16[128,896]{1,0:T(8,128)(2,1)S(1)}, bf16[128,896]{1,0:T(8,128)(2,1)S(1)}, u32[]{:S(2)}, u32[]{:S(2)}) collective-permute-start(bf16[128,896]{1,0:T(8,128)(2,1)S(1)} %add_convert_fusion.5), channel_id=1, source_target_pairs={{0,8},{1,9},{2,10},{3,11},{4,12},{5,13},{6,14},{7,15},{8,0},{9,1},... | collective-permute-start | bytes 688136 | tf_op jit(solution)/shard_map/ppermute | solution.py:65
  148.0 12.7 %collective-permute-start.29 = (bf16[128,896]{1,0:T(8,128)(2,1)S(1)}, bf16[128,896]{1,0:T(8,128)(2,1)S(1)}, u32[]{:S(2)}, u32[]{:S(2)}) collective-permute-start(bf16[128,896]{1,0:T(8,128)(2,1)S(1)} %add_convert_fusion.6), channel_id=1, source_target_pairs={{0,8},{1,9},{2,10},{3,11},{4,12},{5,13},{6,14},{7,15},{8,0},{9,1},... | collective-permute-start | bytes 688136 | tf_op jit(solution)/shard_map/ppermute | solution.py:65
  154.5 11.2 %collective-permute-start.33 = (bf16[128,896]{1,0:T(8,128)(2,1)S(1)}, bf16[128,896]{1,0:T(8,128)(2,1)S(1)}, u32[]{:S(2)}, u32[]{:S(2)}) collective-permute-start(bf16[128,896]{1,0:T(8,128)(2,1)S(1)} %add_convert_fusion.4), channel_id=1, source_target_pairs={{0,16},{1,17},{2,18},{3,19},{4,20},{5,21},{6,22},{7,23},{8,24},{9,... | collective-permute-start | bytes 688136 | tf_op jit(solution)/shard_map/ppermute | solution.py:65
